TPU v7x, 32 devices: a whole 2x2x4 slice. The times are simulated.
32 devices in a mesh: tm: 4 (over z), mp: 4 (over y, x), dec: 2 (over core).
Axes of the slice: x: 2, y: 2, z: 4, core: 2. Of those that a mesh axis runs over, the one named last changes fastest.
Arguments:
- latents: bfloat16 [1024, 3072], P('tm'), may hold values from -6 to 6
- modulation: float32 [4, 3, 3072], P('tm'), may hold values from -1.5 to 3.5
- w_qkv: bfloat16 [3, 3072, 3072], P(None, None, ('mp', 'dec'))
- w_out: bfloat16 [3072, 3072], P(('mp', 'dec')), may hold values from -0.109375 to 0.109375
- block_mask: int32 [4, 4], replicated, may hold values from 0 to 1, as said below
- lengths: int32 [4], replicated, may hold values from 64 to 256, as said below
Outputs:
- updated: bfloat16 [1024, 3072], P('tm', ('mp', 'dec'))
Inputs may be any that keep to these rules, and one draw needn't show every extreme that they name: block_mask[i, i] = 1 and block_mask[i, j] = 0 for j > i. `lengths`: some group of index 2 or more has all 256 tokens live.
All inputs are finite; a program needn't handle non-finite values.
Results may differ from a plain program's by a relative error of at most 0.0057.
Values may be sent and summed in bfloat16 or wider, within the bound.
A program may use at most 192 MiB of HBM per device.

v0:
```python
import jax
import jax.numpy as jnp
from jax import lax
from jax.sharding import PartitionSpec as P

HS = 128


def passed_along(block, axis, distance):
    devices = range(lax.axis_size(axis))
    route = [(i - distance, i) for i in devices if i - distance in devices]
    return lax.ppermute(block, axis, route)


def shards(latents, modulation, w_qkv, w_out, block_mask, lengths):
    tok = latents.shape[0]
    columns = w_qkv.shape[2]
    heads_here = columns // HS
    groups = lengths.shape[0]
    wide = latents.astype(jnp.float32)
    mean = jnp.mean(wide, axis=-1, keepdims=True)
    var = jnp.mean((wide - mean) ** 2, axis=-1, keepdims=True)
    normed = (wide - mean) * lax.rsqrt(var + 1e-06)
    shift_row = modulation[0, 0]
    scale_row = modulation[0, 1]
    gate_row = modulation[0, 2]
    adapted = (normed * (1.0 + scale_row) + shift_row).astype(jnp.bfloat16)
    query = jnp.dot(adapted, w_qkv[0], preferred_element_type=jnp.float32).astype(jnp.bfloat16)
    key = jnp.dot(adapted, w_qkv[1], preferred_element_type=jnp.float32).astype(jnp.bfloat16)
    value = jnp.dot(adapted, w_qkv[2], preferred_element_type=jnp.float32).astype(jnp.bfloat16)
    mine = lax.axis_index("tm")
    mask_row = lax.dynamic_slice_in_dim(block_mask, mine, 1, 0)
    inv_root = 1.0 / jnp.sqrt(jnp.float32(HS))
    group_ids = jnp.arange(groups, dtype=jnp.int32)

    def attend(carry, key_rows, value_rows, start, query_heads, mask_rows):
        count = key_rows.shape[0]
        slots = jnp.arange(count, dtype=jnp.int32)
        key_group = start // tok + slots // tok
        onehot = key_group[:, None] == group_ids[None, :]
        live_len = jnp.sum(onehot.astype(jnp.int32) * lengths[None, :], axis=1)
        wanted = (
            jnp.dot(mask_rows.astype(jnp.float32), jnp.transpose(onehot.astype(jnp.float32))) > 0.5
        )
        allowed = wanted & (slots % tok < live_len)[None, :]

        def update(state):
            peak, total, accum = state
            key_heads = key_rows.reshape(count, heads_here, HS)
            value_heads = value_rows.reshape(count, heads_here, HS)
            score = (
                jnp.einsum(
                    "thd,shd->hts", query_heads, key_heads, preferred_element_type=jnp.float32
                )
                * inv_root
            )
            score = jnp.where(allowed[None, :, :], score, jnp.float32(-1e30))
            fresh = jnp.maximum(peak, jnp.max(score, axis=-1))
            keep = jnp.exp(peak - fresh)
            weight = jnp.exp(score - fresh[:, :, None]) * allowed[None, :, :].astype(jnp.float32)
            total = total * keep + jnp.sum(weight, axis=-1)
            mixed = jnp.einsum(
                "hts,shd->thd",
                weight.astype(jnp.bfloat16),
                value_heads,
                preferred_element_type=jnp.float32,
            )
            accum = accum * jnp.transpose(keep)[:, :, None] + mixed
            return (fresh, total, accum)

        return lax.cond(jnp.any(allowed), update, lambda state: state, carry)

    query_heads = query.reshape(tok, heads_here, HS)
    own_mask = jnp.broadcast_to(mask_row, (tok, groups))
    state = attend(
        (
            jnp.full((heads_here, tok), -1e30, jnp.float32),
            jnp.zeros((heads_here, tok), jnp.float32),
            jnp.zeros((tok, heads_here, HS), jnp.float32),
        ),
        key,
        value,
        mine * tok,
        query_heads,
        own_mask,
    )
    stacked = jnp.stack([key, value])

    def hop_step(hop, loop_carry):
        blocks, inner = loop_carry
        blocks = passed_along(blocks, "tm", 1)
        inner = attend(inner, blocks[0], blocks[1], (mine - hop) * tok, query_heads, own_mask)
        return (blocks, inner)

    stacked, state = lax.fori_loop(1, lax.axis_size("tm"), hop_step, (stacked, state))
    peak, total, accum = state
    attended = (accum / jnp.transpose(total)[:, :, None]).reshape(tok, columns).astype(jnp.bfloat16)
    terms = jnp.dot(attended, w_out, preferred_element_type=jnp.float32)
    summed = lax.psum_scatter(
        terms.astype(jnp.bfloat16), ("mp", "dec"), scatter_dimension=1, tiled=True
    ).astype(jnp.float32)
    share = summed.shape[1]
    offset = lax.axis_index(("mp", "dec")) * share
    wide_here = lax.dynamic_slice_in_dim(wide, offset, share, 1)
    gate_here = lax.dynamic_slice_in_dim(gate_row, offset, share, 0)
    return (wide_here + gate_here[None, :] * summed).astype(jnp.bfloat16)


def solution(mesh):
    return jax.shard_map(
        shards,
        mesh=mesh,
        in_specs=(
            P("tm", None),
            P("tm", None, None),
            P(None, None, ("mp", "dec")),
            P(("mp", "dec"), None),
            P(),
            P(),
        ),
        out_specs=P("tm", ("mp", "dec")),
        check_vma=False,
    )
```

profile of v0, /device:TPU:0, one launch (start us, length us, event | category | flops | bytes accessed | tf_op | source)
XLA Modules:
  0.0 129.3 jit_solution(14822240629196739454)
XLA Ops:
  6.5 0.0 copy-start
  6.5 0.0 copy-start.2
  6.5 0.0 reduce-scatter.4.cloned.1.call-start
  6.5 0.0 copy-start.1
  6.5 1.8 %convert_reduce_fusion = f32[256]{0:T(256)S(1)} fusion(bf16[256,3072]{1,0:T(8,128)(2,1)} %param.12), kind=kLoop, calls=%fused_computation.56 | loop fusion | flops 1572608 | bytes 1573888 | tf_op jit(solution)/shard_map/reduce_sum | solution.py:21
  8.4 2.0 %multiply_reduce_fusion = f32[256]{0:T(256)S(1)} fusion(bf16[256,3072]{1,0:T(8,128)(2,1)} %param.12, f32[256]{0:T(256)S(1)} %broadcast_multiply_fusion), kind=kLoop, calls=%fused_computation.46 | loop fusion | flops 3145472 | bytes 1574912 | tf_op jit(solution)/shard_map/reduce_sum | solution.py:22
  10.4 0.0 copy-done.2
  10.4 0.6 fusion.63
  11.0 0.0 copy-done.1
  11.0 0.0 copy-start.4
  11.0 2.9 %fusion.44 = bf16[256,384]{1,0:T(8,128)(2,1)S(1)} fusion(bf16[3,3072,384]{2,1,0:T(8,128)(2,1)} %param.14, bf16[256,3072]{1,0:T(8,128)(2,1)S(1)} %copy-done.1, f32[3072]{0:T(1024)S(1)} %bitcast.66, f32[3072]{0:T(1024)S(1)} %bitcast.69, f32[256]{0:T(256)S(1)} %add_rsqrt_fusion, f32[256]{0:T(256)S(1)} %broadcast_multiply_fusion), kind=kOutput, calls=%fused_computation.58 | convolution fusion | flops 608796672 | bytes 4155392 | tf_op jit(solution)/shard_map/dot_general | solution.py:30
  13.9 0.8 copy-done.4
  14.7 1.1 fusion.41
  15.8 0.0 copy-start.3
  15.8 1.1 fusion.47
  16.9 0.0 copy-done.3
  17.0 0.1 select_reduce_fusion
  17.1 0.7 fusion.58
  17.7 1.5 %fusion.64 = (pred[]{:T(512)}, pred[256,256]{1,0:T(8,128)(4,1)}) fusion(pred[256]{0:T(512)(128)(4,1)S(1)} %fusion.55, s32[256]{0:T(256)S(1)} %fusion.56, bf16[4]{0:T(256)(128)(2,1)S(1)} %fusion.58), kind=kOutput, calls=%fused_computation.90 | convolution fusion | flops 721919 | bytes 66825 | tf_op jit(solution)/shard_map/dot_general | solution.py:43
  20.0 0.1 copy.48
  20.1 0.2 copy.54
  20.3 0.9 copy.53
  21.2 4.8 %conditional.2 = (f32[3,256]{1,0:T(4,128)}, f32[3,256]{1,0:T(4,128)S(1)}, f32[256,3,128]{2,0,1:T(8,128)S(1)}) conditional(s32[]{:T(128)} %convert_element_type.87, () %tuple.45, (pred[256,256]{1,0:T(8,128)(4,1)}, bf16[256,384]{1,0:T(8,128)(2,1)S(1)}, bf16[256,3,128]{0,2,1:T(8,128)(2,1)S(1)}, bf16[256,384]{1,0:T(8,128)(2,1)S(1)}) %tuple.96), branch_computations={%region_4.5_spmd, %region_5.8_spmd} | conditional | flops 102599680 | bytes 5211160 | solution.py:71
  21.2 0.1 copy.52
  21.4 1.0 copy.49
  22.4 0.1 copy.50
  22.6 0.3 fusion.62
  22.9 0.6 fusion.11
  23.5 0.8 fusion.7
  24.3 1.0 fusion.5
  25.4 0.7 fusion.12
  26.1 42.1 %while.23 = (s32[]{:T(128)}, bf16[2,256,384]{1,2,0:T(8,128)(2,1)}, f32[3,256]{1,0:T(4,128)}, f32[3,256]{1,0:T(4,128)S(1)}, f32[256,3,128]{2,0,1:T(8,128)S(1)}, /...) while((s32[]{:T(128)}, bf16[2,256,384]{1,2,0:T(8,128)(2,1)}, ...), condition=%wide.region_15.16_spmd.clone, body=%wide.region_8.15_spmd.clone.sunk | while | flops 103427088 | bytes 7919597 | solution.py:95
  26.1 5.0 %collective-permute-start = (bf16[2,256,384]{1,2,0:T(8,128)(2,1)}, bf16[2,256,384]{1,2,0:T(8,128)(2,1)S(1)}, u32[]{:S(2)}, u32[]{:S(2)}) collective-permute-start(bf16[2,256,384]{1,2,0:T(8,128)(2,1)} %get-tuple-element.560), channel_id=1, source_target_pairs={{0,8},{8,16},{16,24},{1,9},{9,17},{17,25},{2,10},{10,18},{18,26},{... | collective-permute-start | bytes 1179656 | tf_op jit(solution)/shard_map/while/body/eval_jaxpr/ppermute | solution.py:12
  31.1 0.1 fusion.78
  31.2 0.9 fusion.80
  32.7 7.0 %collective-permute-done = bf16[2,256,384]{1,2,0:T(8,128)(2,1)S(1)} collective-permute-done((bf16[2,256,384]{1,2,0:T(8,128)(2,1)}, bf16[2,256,384]{1,2,0:T(8,128)(2,1)S(1)}, u32[]{:S(2)}, u32[]{:S(2)}) %collective-permute-start) | collective-permute-done | bytes 393248 | tf_op jit(solution)/shard_map/while/body/eval_jaxpr/ppermute | solution.py:12
  39.7 0.7 copy.88
  40.4 7.2 %collective-permute-start = (bf16[2,256,384]{1,2,0:T(8,128)(2,1)}, bf16[2,256,384]{1,2,0:T(8,128)(2,1)S(1)}, u32[]{:S(2)}, u32[]{:S(2)}) collective-permute-start(bf16[2,256,384]{1,2,0:T(8,128)(2,1)} %get-tuple-element.560), channel_id=1, source_target_pairs={{0,8},{8,16},{16,24},{1,9},{9,17},{17,25},{2,10},{10,18},{18,26},{... | collective-permute-start | bytes 1179656 | tf_op jit(solution)/shard_map/while/body/eval_jaxpr/ppermute | solution.py:12
  47.7 0.1 fusion.78
  47.8 0.9 fusion.80
  49.4 6.1 %collective-permute-done = bf16[2,256,384]{1,2,0:T(8,128)(2,1)S(1)} collective-permute-done((bf16[2,256,384]{1,2,0:T(8,128)(2,1)}, bf16[2,256,384]{1,2,0:T(8,128)(2,1)S(1)}, u32[]{:S(2)}, u32[]{:S(2)}) %collective-permute-start) | collective-permute-done | bytes 393248 | tf_op jit(solution)/shard_map/while/body/eval_jaxpr/ppermute | solution.py:12
  55.5 0.7 copy.88
  56.2 4.3 %collective-permute-start = (bf16[2,256,384]{1,2,0:T(8,128)(2,1)}, bf16[2,256,384]{1,2,0:T(8,128)(2,1)S(1)}, u32[]{:S(2)}, u32[]{:S(2)}) collective-permute-start(bf16[2,256,384]{1,2,0:T(8,128)(2,1)} %get-tuple-element.560), channel_id=1, source_target_pairs={{0,8},{8,16},{16,24},{1,9},{9,17},{17,25},{2,10},{10,18},{18,26},{... | collective-permute-start | bytes 1179656 | tf_op jit(solution)/shard_map/while/body/eval_jaxpr/ppermute | solution.py:12
  60.5 0.1 fusion.78
  60.6 0.9 fusion.80
  62.2 5.3 %collective-permute-done = bf16[2,256,384]{1,2,0:T(8,128)(2,1)S(1)} collective-permute-done((bf16[2,256,384]{1,2,0:T(8,128)(2,1)}, bf16[2,256,384]{1,2,0:T(8,128)(2,1)S(1)}, u32[]{:S(2)}, u32[]{:S(2)}) %collective-permute-start) | collective-permute-done | bytes 393248 | tf_op jit(solution)/shard_map/while/body/eval_jaxpr/ppermute | solution.py:12
  67.4 0.7 copy.88
  68.2 0.2 copy.55
  68.4 0.0 copy-done
  68.4 2.2 %convolution_convert_fusion = bf16[256,3072]{1,0:T(8,128)(2,1)} fusion(bf16[256,384]{0,1:T(8,128)(2,1)S(1)} %bitcast.59, bf16[384,3072]{1,0:T(8,128)(2,1)S(1)} %copy-done), kind=kOutput, calls=%fused_computation.44 | convolution fusion | flops 604766208 | bytes 4128768 | tf_op jit(solution)/shard_map/dot_general | solution.py:98
  70.6 2.6 %copy.63 = bf16[256,3072]{0,1:T(8,128)(2,1)} copy(bf16[256,3072]{1,0:T(8,128)(2,1)} %convolution_convert_fusion) | data formatting | bytes 3145728
  73.1 0.0 reduce-scatter.4.cloned.1.call-update
  73.2 3.4 %convert_element_type.81 = f32[256,3072]{1,0:T(8,128)} convert(bf16[256,3072]{1,0:T(8,128)(2,1)} %param.12) | non-fusion elementwise | flops 786432 | bytes 4718592 | tf_op jit(solution)/shard_map/convert_element_type | solution.py:20
  76.6 0.7 dynamic-slice_reduce_fusion
  77.3 42.3 %reduce-scatter.4.cloned.1.call-done = bf16[384,256]{1,0:T(8,128)(2,1)} async-done(((bf16[3072,256]{1,0:T(8,128)(2,1)}), bf16[384,256]{1,0:T(8,128)(2,1)}) %reduce-scatter.4.cloned.1.call-update) | async-done | bytes 196624
  119.6 1.1 copy.64
  120.7 1.7 %add_convert_fusion.1 = bf16[256,384]{1,0:T(8,128)(2,1)} fusion(bf16[256,384]{1,0:T(8,128)(2,1)S(1)} %copy.64, f32[256,3072]{1,0:T(8,128)} %convert_element_type.81, s32[]{:T(128)S(6)} %select_n.86, f32[384]{0:T(512)S(1)} %dynamic-slice_reduce_fusion), kind=kLoop, calls=%fused_computation.63 | loop fusion | flops 393216 | bytes 787972 | tf_op jit(solution)/shard_map/convert_element_type | solution.py:106
  (16 shorter events, 0.2 us)
Async XLA Ops:
  6.5 61.9 %copy-start = (bf16[384,3072]{1,0:T(8,128)(2,1)S(1)}, bf16[384,3072]{1,0:T(8,128)(2,1)}, u32[]{:S(2)}) copy-start(bf16[384,3072]{1,0:T(8,128)(2,1)} %param.15) | copy-start | bytes 7077892
  6.5 3.8 %copy-start.2 = (f32[1,3,3072]{2,0,1:T(1,128)S(1)}, f32[1,3,3072]{2,0,1:T(1,128)}, u32[]{:S(2)}) copy-start(f32[1,3,3072]{2,0,1:T(1,128)} %param.13) | copy-start | bytes 110596
  6.5 113.1 %reduce-scatter.4.cloned.1.call-start = ((), (), s32[]{:S(2)}) async-start(), calls=%async_computation.1 | async-start | bytes 1769472
  6.5 4.5 %copy-start.1 = (bf16[256,3072]{1,0:T(8,128)(2,1)S(1)}, bf16[256,3072]{1,0:T(8,128)(2,1)}, u32[]{:S(2)}) copy-start(bf16[256,3072]{1,0:T(8,128)(2,1)} %param.12) | copy-start | bytes 4718596
  11.0 3.7 %copy-start.4 = (bf16[3,3072,384]{2,1,0:T(8,128)(2,1)S(1)}, bf16[3,3072,384]{2,1,0:T(8,128)(2,1)}, u32[]{:S(2)}) copy-start(bf16[3,3072,384]{2,1,0:T(8,128)(2,1)} %param.14) | copy-start | bytes 21233668
  15.8 1.1 copy-start.3
  26.1 13.6 %collective-permute-start = (bf16[2,256,384]{1,2,0:T(8,128)(2,1)}, bf16[2,256,384]{1,2,0:T(8,128)(2,1)S(1)}, u32[]{:S(2)}, u32[]{:S(2)}) collective-permute-start(bf16[2,256,384]{1,2,0:T(8,128)(2,1)} %get-tuple-element.560), channel_id=1, source_target_pairs={{0,8},{8,16},{16,24},{1,9},{9,17},{17,25},{2,10},{10,18},{18,26},{... | collective-permute-start | bytes 1179656 | tf_op jit(solution)/shard_map/while/body/eval_jaxpr/ppermute | solution.py:12
  40.4 15.0 %collective-permute-start = (bf16[2,256,384]{1,2,0:T(8,128)(2,1)}, bf16[2,256,384]{1,2,0:T(8,128)(2,1)S(1)}, u32[]{:S(2)}, u32[]{:S(2)}) collective-permute-start(bf16[2,256,384]{1,2,0:T(8,128)(2,1)} %get-tuple-element.560), channel_id=1, source_target_pairs={{0,8},{8,16},{16,24},{1,9},{9,17},{17,25},{2,10},{10,18},{18,26},{... | collective-permute-start | bytes 1179656 | tf_op jit(solution)/shard_map/while/body/eval_jaxpr/ppermute | solution.py:12
  56.2 11.2 %collective-permute-start = (bf16[2,256,384]{1,2,0:T(8,128)(2,1)}, bf16[2,256,384]{1,2,0:T(8,128)(2,1)S(1)}, u32[]{:S(2)}, u32[]{:S(2)}) collective-permute-start(bf16[2,256,384]{1,2,0:T(8,128)(2,1)} %get-tuple-element.560), channel_id=1, source_target_pairs={{0,8},{8,16},{16,24},{1,9},{9,17},{17,25},{2,10},{10,18},{18,26},{... | collective-permute-start | bytes 1179656 | tf_op jit(solution)/shard_map/while/body/eval_jaxpr/ppermute | solution.py:12
Sparse Core Ops, SparseCore 0:
  73.3 46.2 reduce-scatter.3
where the time goes:
time: 130 us; the launch traced here: 129 us
  waiting for transfers between devices  60.7 us (47%)
  starting transfers between devices  16.5 us (13%)
  between operations  14.2 us (11%)
  other arithmetic  12.9 us (10%)
  matrix products  12.8 us (10%)
  local copies, waits for them, and re-layouts  10.1 us (8%)
  loops' own time  2.12 us (2%)
    unnamed x2, waiting for transfers between devices  42.3 us
    ppermute x3, waiting for transfers between devices, passed_along(): return lax.ppermute(block, axis, route)  18.3 us
    ppermute x3, starting transfers between devices, passed_along(): return lax.ppermute(block, axis, route)  16.5 us
    unnamed x14, local copies, waits for them, and re-layouts  5.57 us
    dot_general x4, matrix products, attend(): jnp.dot(mask_rows.astype(jnp.float32), jnp.transpose(onehot.astype(jnp.fl...  4.2 us
    convert_element_type x1, other arithmetic, shards(): wide = latents.astype(jnp.float32)  3.44 us
    dot_general x1, matrix products, shards(): jnp.dot(adapted, w_qkv[2], preferred_element_type=jnp.float32)  2.9 us
  transfers between devices with their start and end apart: 4, of which 4 were waited for; matrix products, arithmetic and copies ran while one was open for 6% of the time, Pallas kernels for 0%

commit v1 on v0

v1 whole, which is shorter than its diff:
```python
import functools
import math

import jax
import jax.numpy as jnp
from jax import lax
from jax.experimental import pallas as pl
from jax.experimental.pallas import tpu as pltpu
from jax.sharding import PartitionSpec as P

HS = 128
EPS = 1e-6
MESH = pl.DeviceIdType.MESH
F32 = jnp.float32
BF16 = jnp.bfloat16


def kernel(
    sizes,
    lat_hbm,
    mod_ref,
    wqkv_hbm,
    wout_hbm,
    mask_ref,
    len_ref,
    out_ref,
    x,
    adapted,
    w,
    wo,
    q,
    kv,
    peak,
    total,
    accum,
    attended,
    tx1,
    rx1,
    tx2,
    rx2,
    x_sem,
    w_sem,
    wo_sem,
    kv_send,
    kv_recv,
    send1,
    recv1,
    send2,
    recv2,
):
    n, M, D, parts = sizes
    tok, width = x.shape
    columns = q.shape[1]
    heads = columns // HS
    share = out_ref.shape[1]
    depth = width // parts
    mine = lax.axis_index("tm")
    mp = lax.axis_index("mp")
    dec = lax.axis_index("dec")

    def load_w(which, place, part):
        rows = pl.ds(part * depth, depth)
        return pltpu.make_async_copy(
            wqkv_hbm.at[which, rows],
            w.at[rows, pl.ds(place * columns, columns)],
            w_sem.at[place, part],
        )

    load_x = pltpu.make_async_copy(lat_hbm, x, x_sem)
    load_wo = pltpu.make_async_copy(wout_hbm, wo, wo_sem)
    load_x.start()
    for part in range(parts):
        load_w(1, 0, part).start()
        load_w(2, 1, part).start()
    for part in range(parts):
        load_w(0, 2, part).start()
    load_wo.start()

    barrier = pltpu.get_barrier_semaphore()
    right = lax.rem(mine + 1, n)
    left = lax.rem(mine + n - 1, n)
    for other in (left, right):
        pl.semaphore_signal(barrier, inc=1, device_id={"tm": other}, device_id_type=MESH)
    for j in range(1, M):
        pl.semaphore_signal(
            barrier, inc=1, device_id={"mp": lax.rem(mp + j, M)}, device_id_type=MESH
        )
    for d in range(1, D):
        pl.semaphore_signal(
            barrier, inc=1, device_id={"dec": lax.rem(dec + d, D)}, device_id_type=MESH
        )

    load_x.wait()
    shift = mod_ref[0, 0:1, :]
    scale = 1.0 + mod_ref[0, 1:2, :]
    step = 16

    def norm(i, carry):
        rows = pl.ds(pl.multiple_of(i * step, step), step)
        wide = x[rows, :].astype(F32)
        mean = jnp.sum(wide, axis=-1, keepdims=True) * (1.0 / width)
        centred = wide - mean
        var = jnp.sum(centred * centred, axis=-1, keepdims=True) * (1.0 / width)
        adapted[rows, :] = (centred * lax.rsqrt(var + EPS) * scale + shift).astype(BF16)
        return carry

    lax.fori_loop(0, tok // step, norm, 0)

    def project(first, count):
        out = None
        for part in range(parts):
            for place in range(first, first + count):
                load_w((1, 2, 0)[place], place, part).wait()
            rows = pl.ds(part * depth, depth)
            piece = jnp.dot(
                adapted[:, rows],
                w[rows, pl.ds(first * columns, count * columns)],
                preferred_element_type=F32,
            )
            out = piece if out is None else out + piece
        return out.astype(BF16)

    def pass_on(hop, head):
        return pltpu.make_async_remote_copy(
            src_ref=kv.at[hop - 1, head],
            dst_ref=kv.at[hop, head],
            send_sem=kv_send.at[hop - 1, head],
            recv_sem=kv_recv.at[hop - 1, head],
            device_id={"tm": right},
            device_id_type=MESH,
        )

    own = project(0, 2)
    for head in range(heads):
        kv[0, head, 0] = own[:, head * HS : (head + 1) * HS]
        kv[0, head, 1] = own[:, columns + head * HS : columns + (head + 1) * HS]
    pl.semaphore_wait(barrier, 2 + (M - 1) + (D - 1))

    @pl.when(mine + 1 < n)
    def _():
        for head in range(heads):
            pass_on(1, head).start()

    q[...] = project(2, 1)
    slots = lax.broadcasted_iota(jnp.int32, (1, tok), 1)
    factor = math.log2(math.e) / math.sqrt(HS)

    def scores(hop, head):
        group = mine - hop
        live = jnp.where(mask_ref[mine, group] == 1, len_ref[group], 0)
        score = lax.dot_general(
            q[:, head * HS : (head + 1) * HS],
            kv[hop, head, 0],
            (((1,), (1,)), ((), ())),
            preferred_element_type=F32,
        )
        return jnp.where(slots < live, score * factor, -1e30)

    for head in range(heads):
        score = scores(0, head)
        top = jnp.max(score, axis=-1, keepdims=True)
        weight = jnp.exp2(score - top)
        peak[head] = top
        total[head] = jnp.sum(weight, axis=-1, keepdims=True)
        accum[head] = jnp.dot(
            weight.astype(BF16), kv[0, head, 1], preferred_element_type=F32
        )

    def hop_step(hop, carry):
        @pl.when(mine >= hop)
        def _():
            for head in range(heads):
                pass_on(hop, head).wait_recv()

                @pl.when((mine + 1 < n) & (hop + 1 < n))
                def _():
                    pass_on(hop + 1, head).start()

                score = scores(hop, head)
                old = peak[head]
                top = jnp.maximum(old, jnp.max(score, axis=-1, keepdims=True))
                keep = jnp.exp2(old - top)
                weight = jnp.exp2(score - top)
                peak[head] = top
                total[head] = total[head] * keep + jnp.sum(weight, axis=-1, keepdims=True)
                accum[head] = accum[head] * keep + jnp.dot(
                    weight.astype(BF16), kv[hop, head, 1], preferred_element_type=F32
                )

        return carry

    lax.fori_loop(1, n, hop_step, 0)
    for head in range(heads):
        attended[:, head * HS : (head + 1) * HS] = (accum[head] / total[head]).astype(BF16)
    load_wo.wait()

    def term(chip, core):
        start = pl.multiple_of((chip * D + core) * share, share)
        return jnp.dot(attended[...], wo[:, pl.ds(start, share)], preferred_element_type=F32)

    def to_core(d, j):
        return pltpu.make_async_remote_copy(
            src_ref=tx1.at[d - 1, j],
            dst_ref=rx1.at[d - 1, j],
            send_sem=send1.at[d - 1, j],
            recv_sem=recv1.at[d - 1, j],
            device_id={"dec": lax.rem(dec + d, D)},
            device_id_type=MESH,
        )

    def to_chip(j):
        return pltpu.make_async_remote_copy(
            src_ref=tx2.at[j - 1],
            dst_ref=rx2.at[j - 1],
            send_sem=send2.at[j - 1],
            recv_sem=recv2.at[j - 1],
            device_id={"mp": lax.rem(mp + j, M)},
            device_id_type=MESH,
        )

    order = list(range(1, M)) + [0]
    for j in order:
        for d in range(1, D):
            tx1[d - 1, j] = term(lax.rem(mp + j, M), lax.rem(dec + d, D)).astype(BF16)
            to_core(d, j).start()
    for j in order:
        part = term(lax.rem(mp + j, M), dec)
        for d in range(1, D):
            to_core(d, j).wait_recv()
            part = part + rx1[d - 1, j].astype(F32)
        if j > 0:
            tx2[j - 1] = part.astype(BF16)
            to_chip(j).start()
    for j in range(1, M):
        to_chip(j).wait_recv()
        part = part + rx2[j - 1].astype(F32)
    mine_columns = pl.ds(pl.multiple_of((mp * D + dec) * share, share), share)
    gate = mod_ref[0, 2:3, mine_columns]
    out_ref[...] = (x[:, mine_columns].astype(F32) + gate * part).astype(BF16)

    for j in order:
        for d in range(1, D):
            to_core(d, j).wait_send()
    for j in range(1, M):
        to_chip(j).wait_send()

    def sent(hop, carry):
        @pl.when((mine + 1 < n) & (mine >= hop - 1))
        def _():
            for head in range(heads):
                pass_on(hop, head).wait_send()

        return carry

    lax.fori_loop(1, n, sent, 0)


def solution(mesh):
    n, M, D = mesh.shape["tm"], mesh.shape["mp"], mesh.shape["dec"]

    def shards(latents, modulation, w_qkv, w_out, block_mask, lengths):
        tok, width = latents.shape
        columns = w_qkv.shape[2]
        heads = columns // HS
        share = width // (M * D)
        parts = 3
        vmem = pl.BlockSpec(memory_space=pltpu.VMEM)
        smem = pl.BlockSpec(memory_space=pltpu.SMEM)
        anywhere = pl.BlockSpec(memory_space=pl.ANY)
        dma = pltpu.SemaphoreType.DMA
        return pl.pallas_call(
            functools.partial(kernel, (n, M, D, parts)),
            out_shape=jax.ShapeDtypeStruct((tok, share), BF16),
            in_specs=[anywhere, vmem, anywhere, anywhere, smem, smem],
            out_specs=vmem,
            scratch_shapes=[
                pltpu.VMEM((tok, width), BF16),
                pltpu.VMEM((tok, width), BF16),
                pltpu.VMEM((width, 3 * columns), BF16),
                pltpu.VMEM((columns, width), BF16),
                pltpu.VMEM((tok, columns), BF16),
                pltpu.VMEM((n, heads, 2, tok, HS), BF16),
                pltpu.VMEM((heads, tok, 1), F32),
                pltpu.VMEM((heads, tok, 1), F32),
                pltpu.VMEM((heads, tok, HS), F32),
                pltpu.VMEM((tok, columns), BF16),
                pltpu.VMEM((D - 1, M, tok, share), BF16),
                pltpu.VMEM((D - 1, M, tok, share), BF16),
                pltpu.VMEM((M - 1, tok, share), BF16),
                pltpu.VMEM((M - 1, tok, share), BF16),
                dma,
                dma((3, parts)),
                dma,
                dma((n - 1, heads)),
                dma((n - 1, heads)),
                dma((D - 1, M)),
                dma((D - 1, M)),
                dma((M - 1,)),
                dma((M - 1,)),
            ],
            compiler_params=pltpu.CompilerParams(collective_id=0, has_side_effects=True),
        )(latents, modulation, w_qkv, w_out, block_mask, lengths)

    return jax.shard_map(
        shards,
        mesh=mesh,
        in_specs=(
            P("tm", None),
            P("tm", None, None),
            P(None, None, ("mp", "dec")),
            P(("mp", "dec"), None),
            P(),
            P(),
        ),
        out_specs=P("tm", ("mp", "dec")),
        check_vma=False,
    )
```

time: 130 us -> 55 us (0.42)
  the two profiles are of different devices: /device:TPU:0 before, /device:TPU:25 now
where the time goes in v1:
time: 55 us; the launch traced here: 54.7 us
  Pallas kernels  51.7 us (94%)
  local copies, waits for them, and re-layouts  3.02 us (5%)
    pallas_call x1, Pallas kernels, shards(): pl.pallas_call(functools.partial(kernel, (n, M, D, parts)), out_shape=jax...  51.7 us
    unnamed x2, local copies, waits for them, and re-layouts  3.02 us

profile of v1, /device:TPU:25, one launch (start us, length us, event | category | flops | bytes accessed | tf_op | source)
XLA Modules:
  0.0 54.7 jit_solution(11499115335392347170)
XLA Ops:
  0.0 1.4 %copy.7.mod_ref = f32[1,3,3072]{2,1,0:T(4,128)} copy(f32[1,3,3072]{2,0,1:T(1,128)} %param.7) | data formatting | bytes 73728 | tf_op args[1]
  1.4 51.7 %shard_map.64 = bf16[256,384]{1,0:T(8,128)(2,1)} custom-call(bf16[256,3072]{1,0:T(8,128)(2,1)} %lat_hbm.1, f32[1,3,3072]{2,1,0:T(4,128)} %copy.7.mod_ref, bf16[3,3072,384]{2,1,0:T(8,128)(2,1)} %wqkv_hbm.1, bf16[384,3072]{1,0:T(8,128)(2,1)} %wout_hbm.1, s32[4,4]{1,0:T(4,128)} %mask_ref.1, s32[4]{0:T(128)} %len_ref.1), custom_call_target="tpu_custom_call" | custom-call | tf_op jit(solution)/shard_map/pallas_call | solution.py:271
  53.1 1.6 %copy.9 = bf16[256,384]{1,0:T(8,128)(2,1)} copy(bf16[256,384]{1,0:T(8,128)(2,1)} %shard_map.64) | data formatting | bytes 393216

commit v2 on v1

--- a/solution.py
+++ b/solution.py
@@ -10,6 +10,7 @@
 
 HS = 128
 EPS = 1e-6
+FAR_BYTES = 16 * 2**20
 MESH = pl.DeviceIdType.MESH
 F32 = jnp.float32
 BF16 = jnp.bfloat16
@@ -38,6 +39,8 @@
     rx1,
     tx2,
     rx2,
+    mods,
+    far,
     x_sem,
     w_sem,
     wo_sem,
@@ -47,8 +50,15 @@
     recv1,
     send2,
     recv2,
+    z_send,
+    z_recv,
+    xy_send,
+    xy_recv,
+    core_send,
+    core_recv,
 ):
-    n, M, D, parts = sizes
+    n, M, D, parts, chunks, far_hops = sizes
+    near = n - 1 - far_hops
     tok, width = x.shape
     columns = q.shape[1]
     heads = columns // HS
@@ -66,9 +76,18 @@
             w_sem.at[place, part],
         )
 
-    load_x = pltpu.make_async_copy(lat_hbm, x, x_sem)
+    pieces = M * D
+    eighth = tok // pieces
+    chunk = eighth // chunks
+    place = mp * D + dec
+
+    def load_x(i):
+        rows = pl.ds(pl.multiple_of(i * eighth, eighth), eighth)
+        return pltpu.make_async_copy(lat_hbm.at[rows], x.at[rows], x_sem.at[i])
+
     load_wo = pltpu.make_async_copy(wout_hbm, wo, wo_sem)
-    load_x.start()
+    for i in range(pieces):
+        load_x(lax.rem(place + i, pieces)).start()
     for part in range(parts):
         load_w(1, 0, part).start()
         load_w(2, 1, part).start()
@@ -79,7 +98,10 @@
     barrier = pltpu.get_barrier_semaphore()
     right = lax.rem(mine + 1, n)
     left = lax.rem(mine + n - 1, n)
-    for other in (left, right):
+    others = [left, right]
+    if far_hops:
+        others += [lax.rem(mine + 2, n), lax.rem(mine + n - 2, n)]
+    for other in others:
         pl.semaphore_signal(barrier, inc=1, device_id={"tm": other}, device_id_type=MESH)
     for j in range(1, M):
         pl.semaphore_signal(
@@ -90,30 +112,112 @@
             barrier, inc=1, device_id={"dec": lax.rem(dec + d, D)}, device_id_type=MESH
         )
 
-    load_x.wait()
-    shift = mod_ref[0, 0:1, :]
-    scale = 1.0 + mod_ref[0, 1:2, :]
+    tiles = width // HS
+    for i in range(tiles):
+        mods[0:1, i * HS : (i + 1) * HS] = mod_ref[i : i + 1, :]
+        mods[1:2, i * HS : (i + 1) * HS] = 1.0 + mod_ref[tiles + i : tiles + i + 1, :]
     step = 16
 
     def norm(i, carry):
-        rows = pl.ds(pl.multiple_of(i * step, step), step)
-        wide = x[rows, :].astype(F32)
-        mean = jnp.sum(wide, axis=-1, keepdims=True) * (1.0 / width)
-        centred = wide - mean
-        var = jnp.sum(centred * centred, axis=-1, keepdims=True) * (1.0 / width)
-        adapted[rows, :] = (centred * lax.rsqrt(var + EPS) * scale + shift).astype(BF16)
+        piece = lax.rem(place + i, pieces)
+        load_x(piece).wait()
+        for at in range(0, eighth, step):
+            rows = pl.ds(pl.multiple_of(piece * eighth + at, step), step)
+            wide = x[rows, :].astype(F32)
+            mean = jnp.sum(wide, axis=-1, keepdims=True) * (1.0 / width)
+            centred = wide - mean
+            var = jnp.sum(centred * centred, axis=-1, keepdims=True) * (1.0 / width)
+            adapted[rows, :] = (
+                centred * lax.rsqrt(var + EPS) * mods[1:2, :] + mods[0:1, :]
+            ).astype(BF16)
         return carry
 
-    lax.fori_loop(0, tok // step, norm, 0)
-
-    def project(first, count):
+    def piece_rows(chip, core, c):
+        start = (chip * D + core) * eighth + c * chunk
+        return pl.ds(pl.multiple_of(start, chunk), chunk)
+
+    def along(hop, c):
+        rows = piece_rows(mp, dec, c)
+        return pltpu.make_async_remote_copy(
+            src_ref=adapted.at[rows] if hop == 2 else far.at[hop - 3, rows],
+            dst_ref=far.at[hop - 2, rows],
+            send_sem=z_send.at[hop - 2, c],
+            recv_sem=z_recv.at[hop - 2, c],
+            device_id={"tm": lax.rem(mine + 2, n) if hop == 2 else right},
+            device_id_type=MESH,
+        )
+
+    def across(hop, j, c, sender):
+        rows = piece_rows(sender, dec, c)
+        return pltpu.make_async_remote_copy(
+            src_ref=far.at[hop - 2, rows],
+            dst_ref=far.at[hop - 2, rows],
+            send_sem=xy_send.at[hop - 2, j - 1, c],
+            recv_sem=xy_recv.at[hop - 2, j - 1, c],
+            device_id={"mp": lax.rem(mp + j, M)},
+            device_id_type=MESH,
+        )
+
+    def to_partner(hop, d, j, c, core):
+        rows = piece_rows(lax.rem(mp + M - j, M), core, c)
+        return pltpu.make_async_remote_copy(
+            src_ref=far.at[hop - 2, rows],
+            dst_ref=far.at[hop - 2, rows],
+            send_sem=core_send.at[hop - 2, d - 1, j, c],
+            recv_sem=core_recv.at[hop - 2, d - 1, j, c],
+            device_id={"dec": lax.rem(dec + d, D)},
+            device_id_type=MESH,
+        )
+
+    def advance(hop, c):
+        if hop - 1 > far_hops:
+            return
+
+        @pl.when(mine >= hop)
+        def _():
+            along(hop, c).wait_recv()
+            if hop + 1 < n:
+
+                @pl.when(mine + 1 < n)
+                def _():
+                    along(hop + 1, c).start()
+
+            for j in range(1, M):
+                across(hop, j, c, mp).start()
+            for d in range(1, D):
+                to_partner(hop, d, 0, c, dec).start()
+
+    def collect(hop, c):
+        if hop - 1 > far_hops:
+            return
+
+        @pl.when(mine >= hop)
+        def _():
+            for j in range(1, M):
+                across(hop, j, c, lax.rem(mp + M - j, M)).wait_recv()
+                for d in range(1, D):
+                    to_partner(hop, d, j, c, dec).start()
+
+    lax.fori_loop(0, 1, norm, 0)
+    pl.semaphore_wait(barrier, len(others) + (M - 1) + (D - 1))
+    if far_hops:
+
+        @pl.when(mine + 2 < n)
+        def _():
+            for c in range(chunks):
+                along(2, c).start()
+
+    lax.fori_loop(1, pieces, norm, 0)
+
+    def project(first, count, source, loading):
         out = None
         for part in range(parts):
-            for place in range(first, first + count):
-                load_w((1, 2, 0)[place], place, part).wait()
+            if loading:
+                for at in range(first, first + count):
+                    load_w((1, 2, 0)[at], at, part).wait()
             rows = pl.ds(part * depth, depth)
             piece = jnp.dot(
-                adapted[:, rows],
+                source[:, rows],
                 w[rows, pl.ds(first * columns, count * columns)],
                 preferred_element_type=F32,
             )
@@ -130,18 +234,22 @@
             device_id_type=MESH,
         )
 
-    own = project(0, 2)
-    for head in range(heads):
-        kv[0, head, 0] = own[:, head * HS : (head + 1) * HS]
-        kv[0, head, 1] = own[:, columns + head * HS : columns + (head + 1) * HS]
-    pl.semaphore_wait(barrier, 2 + (M - 1) + (D - 1))
-
-    @pl.when(mine + 1 < n)
-    def _():
+    def keep_kv(slot, block):
         for head in range(heads):
-            pass_on(1, head).start()
-
-    q[...] = project(2, 1)
+            kv[slot, head, 0] = block[:, head * HS : (head + 1) * HS]
+            kv[slot, head, 1] = block[:, columns + head * HS : columns + (head + 1) * HS]
+
+    def send_own(first, last):
+        @pl.when(mine + 1 < n)
+        def _():
+            for head in range(first, last):
+                pass_on(1, head).start()
+
+    keep_kv(0, project(0, 2, adapted, True))
+    for c in range(chunks - 1):
+        advance(2, c)
+    send_own(0, 1)
+    q[...] = project(2, 1, adapted, True)
     slots = lax.broadcasted_iota(jnp.int32, (1, tok), 1)
     factor = math.log2(math.e) / math.sqrt(HS)
 
@@ -166,30 +274,63 @@
             weight.astype(BF16), kv[0, head, 1], preferred_element_type=F32
         )
 
-    def hop_step(hop, carry):
+    def update(hop, head):
+        score = scores(hop, head)
+        old = peak[head]
+        top = jnp.maximum(old, jnp.max(score, axis=-1, keepdims=True))
+        keep = jnp.exp2(old - top)
+        weight = jnp.exp2(score - top)
+        peak[head] = top
+        total[head] = total[head] * keep + jnp.sum(weight, axis=-1, keepdims=True)
+        accum[head] = accum[head] * keep + jnp.dot(
+            weight.astype(BF16), kv[hop, head, 1], preferred_element_type=F32
+        )
+
+    advance(2, chunks - 1)
+    send_own(1, heads)
+    for c in range(chunks):
+        advance(3, c)
+        collect(2, c)
+
+    def far_step(hop):
+        if hop - 1 > far_hops:
+            return
+
+        @pl.when(mine >= hop)
+        def _():
+            for c in range(chunks):
+                for d in range(1, D):
+                    core = lax.rem(dec + D - d, D)
+                    for j in range(M):
+                        to_partner(hop, d, j, c, core).wait_recv()
+            keep_kv(hop, project(0, 2, far.at[hop - 2], False))
+            for head in range(heads):
+                update(hop, head)
+
+    far_step(2)
+
+    def near_step(hop, carry):
         @pl.when(mine >= hop)
         def _():
             for head in range(heads):
                 pass_on(hop, head).wait_recv()
 
-                @pl.when((mine + 1 < n) & (hop + 1 < n))
+                @pl.when((mine + 1 < n) & (hop < near))
                 def _():
                     pass_on(hop + 1, head).start()
 
-                score = scores(hop, head)
-                old = peak[head]
-                top = jnp.maximum(old, jnp.max(score, axis=-1, keepdims=True))
-                keep = jnp.exp2(old - top)
-                weight = jnp.exp2(score - top)
-                peak[head] = top
-                total[head] = total[head] * keep + jnp.sum(weight, axis=-1, keepdims=True)
-                accum[head] = accum[head] * keep + jnp.dot(
-                    weight.astype(BF16), kv[hop, head, 1], preferred_element_type=F32
-                )
+                update(hop, head)
 
         return carry
 
-    lax.fori_loop(1, n, hop_step, 0)
+    lax.fori_loop(1, near + 1, near_step, 0)
+    for hop in range(3, far_hops + 2):
+        if hop > 3:
+            for c in range(chunks):
+                advance(hop, c)
+        for c in range(chunks):
+            collect(hop, c)
+        far_step(hop)
     for head in range(heads):
         attended[:, head * HS : (head + 1) * HS] = (accum[head] / total[head]).astype(BF16)
     load_wo.wait()
@@ -235,7 +376,10 @@
         to_chip(j).wait_recv()
         part = part + rx2[j - 1].astype(F32)
     mine_columns = pl.ds(pl.multiple_of((mp * D + dec) * share, share), share)
-    gate = mod_ref[0, 2:3, mine_columns]
+    first = 2 * tiles + place * (share // HS)
+    gate = jnp.concatenate(
+        [mod_ref[pl.ds(first + i, 1), :] for i in range(share // HS)], axis=1
+    )
     out_ref[...] = (x[:, mine_columns].astype(F32) + gate * part).astype(BF16)
 
     for j in order:
@@ -252,7 +396,23 @@
 
         return carry
 
-    lax.fori_loop(1, n, sent, 0)
+    lax.fori_loop(1, near + 1, sent, 0)
+    for hop in range(2, far_hops + 2):
+        reach = mine + 2 < n if hop == 2 else (mine + 1 < n) & (mine >= hop - 1)
+
+        @pl.when(reach)
+        def _():
+            for c in range(chunks):
+                along(hop, c).wait_send()
+
+        @pl.when(mine >= hop)
+        def _():
+            for c in range(chunks):
+                for j in range(1, M):
+                    across(hop, j, c, mp).wait_send()
+                for j in range(M):
+                    for d in range(1, D):
+                        to_partner(hop, d, j, c, dec).wait_send()
 
 
 def solution(mesh):
@@ -264,12 +424,16 @@
         heads = columns // HS
         share = width // (M * D)
         parts = 3
+        chunks = 2
+        tiles = width // HS
+        far_hops = n - 2 if (n - 2) * tok * width * 2 <= FAR_BYTES else 0
+        slots = max(far_hops, 1)
         vmem = pl.BlockSpec(memory_space=pltpu.VMEM)
         smem = pl.BlockSpec(memory_space=pltpu.SMEM)
         anywhere = pl.BlockSpec(memory_space=pl.ANY)
         dma = pltpu.SemaphoreType.DMA
         return pl.pallas_call(
-            functools.partial(kernel, (n, M, D, parts)),
+            functools.partial(kernel, (n, M, D, parts, chunks, far_hops)),
             out_shape=jax.ShapeDtypeStruct((tok, share), BF16),
             in_specs=[anywhere, vmem, anywhere, anywhere, smem, smem],
             out_specs=vmem,
@@ -288,7 +452,9 @@
                 pltpu.VMEM((D - 1, M, tok, share), BF16),
                 pltpu.VMEM((M - 1, tok, share), BF16),
                 pltpu.VMEM((M - 1, tok, share), BF16),
-                dma,
+                pltpu.VMEM((2, width), F32),
+                pltpu.VMEM((slots, tok if far_hops else 16, width), BF16),
+                dma((M * D,)),
                 dma((3, parts)),
                 dma,
                 dma((n - 1, heads)),
@@ -297,9 +463,15 @@
                 dma((D - 1, M)),
                 dma((M - 1,)),
                 dma((M - 1,)),
+                dma((slots, chunks)),
+                dma((slots, chunks)),
+                dma((slots, M - 1, chunks)),
+                dma((slots, M - 1, chunks)),
+                dma((slots, D - 1, M, chunks)),
+                dma((slots, D - 1, M, chunks)),
             ],
             compiler_params=pltpu.CompilerParams(collective_id=0, has_side_effects=True),
-        )(latents, modulation, w_qkv, w_out, block_mask, lengths)
+        )(latents, modulation.reshape(3 * tiles, HS), w_qkv, w_out, block_mask, lengths)
 
     return jax.shard_map(
         shards,

time: 55 us -> 49.7 us (0.904)
  Pallas kernels: 51.7 us -> 47.9 us
  local copies, waits for them, and re-layouts: 3.02 us -> 1.62 us
    pallas_call x1, Pallas kernels: 51.7 us -> 47.9 us  [shards(): pl.pallas_call(functools.partial(kernel, (n, M, D, parts, chunks, far_hop...]
    unnamed x2 -> x1, local copies, waits for them, and re-layouts: 3.02 us -> 1.62 us
where the time goes in v2:
time: 49.7 us; the launch traced here: 49.5 us
  Pallas kernels  47.9 us (96%)
  local copies, waits for them, and re-layouts  1.62 us (3%)
    pallas_call x1, Pallas kernels, shards(): pl.pallas_call(functools.partial(kernel, (n, M, D, parts, chunks, far_hop...  47.9 us
    unnamed x1, local copies, waits for them, and re-layouts  1.62 us

profile of v2, /device:TPU:25, one launch (start us, length us, event | category | flops | bytes accessed | tf_op | source)
XLA Modules:
  0.0 49.5 jit_solution(14907105240773602914)
XLA Ops:
  0.0 47.9 %shard_map.64 = bf16[256,384]{1,0:T(8,128)(2,1)} custom-call(bf16[256,3072]{1,0:T(8,128)(2,1)} %lat_hbm.1, f32[72,128]{1,0:T(8,128)} %bitcast.1, bf16[3,3072,384]{2,1,0:T(8,128)(2,1)} %wqkv_hbm.1, bf16[384,3072]{1,0:T(8,128)(2,1)} %wout_hbm.1, s32[4,4]{1,0:T(4,128)} %mask_ref.1, s32[4]{0:T(128)} %len_ref.1), custom_call_target="tpu_custom_call" | custom-call | tf_op jit(solution)/shard_map/pallas_call | solution.py:435
  47.9 1.6 %copy.8 = bf16[256,384]{1,0:T(8,128)(2,1)} copy(bf16[256,384]{1,0:T(8,128)(2,1)} %shard_map.64) | data formatting | bytes 393216

commit v3 on v2

--- a/solution.py
+++ b/solution.py
@@ -147,19 +147,24 @@
             device_id_type=MESH,
         )
 
-    def across(hop, j, c, sender):
-        rows = piece_rows(sender, dec, c)
+    x_chip = mp + 1 - 2 * lax.rem(mp, 2)
+    y_chip = lax.rem(mp + 2, M)
+    chips = (mp, x_chip, y_chip, lax.rem(x_chip + 2, M))
+
+    def across(hop, j, c, origin):
+        rows = piece_rows(chips[origin], dec, c)
+        along_x = j == 1 or (j == 3 and c % 2 == 1)
         return pltpu.make_async_remote_copy(
             src_ref=far.at[hop - 2, rows],
             dst_ref=far.at[hop - 2, rows],
             send_sem=xy_send.at[hop - 2, j - 1, c],
             recv_sem=xy_recv.at[hop - 2, j - 1, c],
-            device_id={"mp": lax.rem(mp + j, M)},
+            device_id={"mp": x_chip if along_x else y_chip},
             device_id_type=MESH,
         )
 
     def to_partner(hop, d, j, c, core):
-        rows = piece_rows(lax.rem(mp + M - j, M), core, c)
+        rows = piece_rows(chips[j], core, c)
         return pltpu.make_async_remote_copy(
             src_ref=far.at[hop - 2, rows],
             dst_ref=far.at[hop - 2, rows],
@@ -182,21 +187,37 @@
                 def _():
                     along(hop + 1, c).start()
 
-            for j in range(1, M):
-                across(hop, j, c, mp).start()
+            for j in (1, 2):
+                across(hop, j, c, 0).start()
             for d in range(1, D):
                 to_partner(hop, d, 0, c, dec).start()
 
-    def collect(hop, c):
+    def via(c):
+        return 1 + c % 2
+
+    def relay(hop):
         if hop - 1 > far_hops:
             return
 
         @pl.when(mine >= hop)
         def _():
-            for j in range(1, M):
-                across(hop, j, c, lax.rem(mp + M - j, M)).wait_recv()
+            for c in range(chunks):
+                across(hop, via(c), c, via(c)).wait_recv()
+                across(hop, 3, c, via(c)).start()
                 for d in range(1, D):
-                    to_partner(hop, d, j, c, dec).start()
+                    to_partner(hop, d, via(c), c, dec).start()
+
+    def collect(hop):
+        if hop - 1 > far_hops:
+            return
+
+        @pl.when(mine >= hop)
+        def _():
+            for c in range(chunks):
+                for j in (3 - via(c), 3):
+                    across(hop, j, c, j).wait_recv()
+                    for d in range(1, D):
+                        to_partner(hop, d, j, c, dec).start()
 
     lax.fori_loop(0, 1, norm, 0)
     pl.semaphore_wait(barrier, len(others) + (M - 1) + (D - 1))
@@ -288,9 +309,10 @@
 
     advance(2, chunks - 1)
     send_own(1, heads)
+    relay(2)
     for c in range(chunks):
         advance(3, c)
-        collect(2, c)
+    collect(2)
 
     def far_step(hop):
         if hop - 1 > far_hops:
@@ -308,6 +330,7 @@
                 update(hop, head)
 
     far_step(2)
+    relay(3)
 
     def near_step(hop, carry):
         @pl.when(mine >= hop)
@@ -328,8 +351,8 @@
         if hop > 3:
             for c in range(chunks):
                 advance(hop, c)
-        for c in range(chunks):
-            collect(hop, c)
+            relay(hop)
+        collect(hop)
         far_step(hop)
     for head in range(heads):
         attended[:, head * HS : (head + 1) * HS] = (accum[head] / total[head]).astype(BF16)
@@ -408,8 +431,9 @@
         @pl.when(mine >= hop)
         def _():
             for c in range(chunks):
-                for j in range(1, M):
-                    across(hop, j, c, mp).wait_send()
+                for j in (1, 2):
+                    across(hop, j, c, 0).wait_send()
+                across(hop, 3, c, via(c)).wait_send()
                 for j in range(M):
                     for d in range(1, D):
                         to_partner(hop, d, j, c, dec).wait_send()
@@ -426,7 +450,7 @@
         parts = 3
         chunks = 2
         tiles = width // HS
-        far_hops = n - 2 if (n - 2) * tok * width * 2 <= FAR_BYTES else 0
+        far_hops = n - 2 if M == 4 and (n - 2) * tok * width * 2 <= FAR_BYTES else 0
         slots = max(far_hops, 1)
         vmem = pl.BlockSpec(memory_space=pltpu.VMEM)
         smem = pl.BlockSpec(memory_space=pltpu.SMEM)

time: 49.7 us -> 50.2 us (1.010)
    pallas_call x1, Pallas kernels: 47.9 us -> 48.4 us  [shards(): pl.pallas_call(functools.partial(kernel, (n, M, D, parts, chunks, far_hop...]
where the time goes in v3:
time: 50.2 us; the launch traced here: 50 us
  Pallas kernels  48.4 us (96%)
  local copies, waits for them, and re-layouts  1.62 us (3%)
    pallas_call x1, Pallas kernels, shards(): pl.pallas_call(functools.partial(kernel, (n, M, D, parts, chunks, far_hop...  48.4 us
    unnamed x1, local copies, waits for them, and re-layouts  1.62 us

profile of v3, /device:TPU:25, one launch (start us, length us, event | category | flops | bytes accessed | tf_op | source)
XLA Modules:
  0.0 50.0 jit_solution(10985019221980109366)
XLA Ops:
  0.0 48.4 %shard_map.64 = bf16[256,384]{1,0:T(8,128)(2,1)} custom-call(bf16[256,3072]{1,0:T(8,128)(2,1)} %lat_hbm.1, f32[72,128]{1,0:T(8,128)} %bitcast.1, bf16[3,3072,384]{2,1,0:T(8,128)(2,1)} %wqkv_hbm.1, bf16[384,3072]{1,0:T(8,128)(2,1)} %wout_hbm.1, s32[4,4]{1,0:T(4,128)} %mask_ref.1, s32[4]{0:T(128)} %len_ref.1), custom_call_target="tpu_custom_call" | custom-call | tf_op jit(solution)/shard_map/pallas_call | solution.py:459
  48.4 1.6 %copy.8 = bf16[256,384]{1,0:T(8,128)(2,1)} copy(bf16[256,384]{1,0:T(8,128)(2,1)} %shard_map.64) | data formatting | bytes 393216

commit v4 on v3

--- a/solution.py
+++ b/solution.py
@@ -88,12 +88,6 @@
     load_wo = pltpu.make_async_copy(wout_hbm, wo, wo_sem)
     for i in range(pieces):
         load_x(lax.rem(place + i, pieces)).start()
-    for part in range(parts):
-        load_w(1, 0, part).start()
-        load_w(2, 1, part).start()
-    for part in range(parts):
-        load_w(0, 2, part).start()
-    load_wo.start()
 
     barrier = pltpu.get_barrier_semaphore()
     right = lax.rem(mine + 1, n)
@@ -221,14 +215,24 @@
 
     lax.fori_loop(0, 1, norm, 0)
     pl.semaphore_wait(barrier, len(others) + (M - 1) + (D - 1))
+
+    def start_far(which):
+        @pl.when(which & (mine + 2 < n))
+        def _():
+            for c in range(chunks):
+                along(2, c).start()
+
     if far_hops:
-
-        @pl.when(mine + 2 < n)
-        def _():
-            for c in range(chunks):
-                along(2, c).start()
-
+        start_far(mine == 0)
+    for part in range(parts):
+        load_w(1, 0, part).start()
+        load_w(2, 1, part).start()
+    for part in range(parts):
+        load_w(0, 2, part).start()
+    load_wo.start()
     lax.fori_loop(1, pieces, norm, 0)
+    if far_hops:
+        start_far(mine > 0)
 
     def project(first, count, source, loading):
         out = None
@@ -271,6 +275,10 @@
         advance(2, c)
     send_own(0, 1)
     q[...] = project(2, 1, adapted, True)
+    advance(2, chunks - 1)
+    send_own(1, heads)
+    for c in range(chunks):
+        advance(3, c)
     slots = lax.broadcasted_iota(jnp.int32, (1, tok), 1)
     factor = math.log2(math.e) / math.sqrt(HS)
 
@@ -307,11 +315,8 @@
             weight.astype(BF16), kv[hop, head, 1], preferred_element_type=F32
         )
 
-    advance(2, chunks - 1)
-    send_own(1, heads)
     relay(2)
-    for c in range(chunks):
-        advance(3, c)
+    relay(3)
     collect(2)
 
     def far_step(hop):
@@ -330,7 +335,6 @@
                 update(hop, head)
 
     far_step(2)
-    relay(3)
 
     def near_step(hop, carry):
         @pl.when(mine >= hop)

time: 50.2 us -> 52.4 us (1.044)
  Pallas kernels: 48.4 us -> 50.5 us
    pallas_call x1, Pallas kernels: 48.4 us -> 50.5 us  [shards(): pl.pallas_call(functools.partial(kernel, (n, M, D, parts, chunks, far_hop...]
where the time goes in v4:
time: 52.4 us; the launch traced here: 52.1 us
  Pallas kernels  50.5 us (96%)
  local copies, waits for them, and re-layouts  1.62 us (3%)
    pallas_call x1, Pallas kernels, shards(): pl.pallas_call(functools.partial(kernel, (n, M, D, parts, chunks, far_hop...  50.5 us
    unnamed x1, local copies, waits for them, and re-layouts  1.62 us

profile of v4, /device:TPU:25, one launch (start us, length us, event | category | flops | bytes accessed | tf_op | source)
XLA Modules:
  0.0 52.1 jit_solution(16330474852986898541)
XLA Ops:
  0.0 50.5 %shard_map.64 = bf16[256,384]{1,0:T(8,128)(2,1)} custom-call(bf16[256,3072]{1,0:T(8,128)(2,1)} %lat_hbm.1, f32[72,128]{1,0:T(8,128)} %bitcast.1, bf16[3,3072,384]{2,1,0:T(8,128)(2,1)} %wqkv_hbm.1, bf16[384,3072]{1,0:T(8,128)(2,1)} %wout_hbm.1, s32[4,4]{1,0:T(4,128)} %mask_ref.1, s32[4]{0:T(128)} %len_ref.1), custom_call_target="tpu_custom_call" | custom-call | tf_op jit(solution)/shard_map/pallas_call | solution.py:463
  50.5 1.6 %copy.8 = bf16[256,384]{1,0:T(8,128)(2,1)} copy(bf16[256,384]{1,0:T(8,128)(2,1)} %shard_map.64) | data formatting | bytes 393216
